TPU v7x, 256 devices: a whole 4x4x8 slice. The times are simulated.
256 devices in a mesh: grp: 4 (over x), wide: 64 (over y, z, core).
Axes of the slice: x: 4, y: 4, z: 8, core: 2. Of those that a mesh axis runs over, the one named last changes fastest.
Arguments:
- spectral: float32 [8, 48, 320, 2, 641], P(None, 'grp', 'wide'), may hold values from -0.006 to 0.006
- legendre: float32 [320, 641, 320], P('wide'), may hold values from -18 to 18
- pair_table: int32 [320], replicated, may hold values from 0 to 319, each once
- field_map: int32 [8], replicated, may hold values from 0 to 7, each once
Outputs:
- grid_values: float32 [8, 48, 640, 1280], P('grp', None, 'wide')
- checksums: float32 [8, 48], replicated
Inputs may be any that keep to these rules, and one draw needn't show every extreme that they name: Each slot number appears once; slot s holds wavenumbers pair_table[s] and 639 - pair_table[s]. `field_map`: each field appears once.
All inputs are finite; a program needn't handle non-finite values.
Results may differ from a plain program's by a relative error of at most 0.000078.
Values sent between devices are 32-bit elements; how exact they have to be, the bound alone decides.
A program may use at most 256 MiB of HBM per device.

v0:
```python
import math

import jax
import jax.numpy as jnp
from jax import lax
from jax.sharding import PartitionSpec as P

WAVES = 640
LAT = 640
LON = 1280


HIGHEST = lax.Precision.HIGHEST


def from_everyone(value, axis):
    copies = jnp.broadcast_to(value, (lax.axis_size(axis), *value.shape))
    return lax.all_to_all(copies, axis, split_axis=0, concat_axis=0, tiled=True)


def taken_together(value, axis):
    everything = from_everyone(value, axis)
    return jnp.sum(everything, axis=0)


def laid_out(tiles, dim):
    tiles = jnp.moveaxis(tiles, 0, dim)
    dims = tiles.shape
    return tiles.reshape(*dims[:dim], dims[dim] * dims[dim + 1], *dims[dim + 2 :])


def collect(value, axis, dim):
    return laid_out(from_everyone(value, axis), dim)


def legendre_table(legendre, slot_pairs):
    slot_count = legendre.shape[0]
    coeff_count = legendre.shape[1]
    degree = jnp.arange(coeff_count, dtype=jnp.int32)[None, :]
    boundary = (WAVES - slot_pairs)[:, None]
    first_part = degree < boundary
    belong = jnp.stack([first_part, ~first_part], 2).astype(jnp.float32)
    sign_first = jnp.broadcast_to(jnp.where(degree % 2 == 0, 1.0, -1.0), (slot_count, coeff_count))
    sign_second = jnp.where((degree - boundary) % 2 == 0, 1.0, -1.0)
    signs = jnp.stack([sign_first, sign_second], 2).astype(jnp.float32)
    north = belong[..., None] * legendre[:, :, None, :]
    south = (belong * signs)[..., None] * jnp.flip(legendre, -1)[:, :, None, :]
    return jnp.concatenate([north, south], -1)


def legendre_sums(coeffs, table):
    return lax.dot_general(
        coeffs,
        table,
        (((4,), (1,)), ((2,), (0,))),
        precision=HIGHEST,
        preferred_element_type=jnp.float32,
    )


def synthesis_table(pair_table):
    numbers = jnp.stack([pair_table, WAVES - 1 - pair_table], 1)
    columns = jnp.arange(LON, dtype=jnp.int32)
    phases = numbers[:, :, None] * columns % LON
    angles = phases.astype(jnp.float32) * (2.0 * math.pi / LON)
    factor = jnp.where(numbers == 0, 1.0, 2.0).astype(jnp.float32)[:, :, None]
    return jnp.stack([factor * jnp.cos(angles), -factor * jnp.sin(angles)], 1)


def local(spectral, legendre, pair_table, field_map):
    slot_count = legendre.shape[0]
    own_pairs = lax.dynamic_slice_in_dim(
        pair_table, lax.axis_index("wide") * slot_count, slot_count
    )
    ordered = jnp.take(spectral, field_map, axis=0)
    table = legendre_table(legendre, own_pairs)
    fourier = legendre_sums(ordered, table)
    arrived = lax.all_to_all(
        lax.all_to_all(fourier, "grp", split_axis=1, concat_axis=2, tiled=True),
        "wide",
        split_axis=5,
        concat_axis=0,
        tiled=True,
    )
    synthesis = synthesis_table(pair_table)
    gridded = lax.dot_general(
        arrived,
        synthesis,
        (((0, 3, 4), (0, 1, 2)), ((), ())),
        precision=HIGHEST,
        preferred_element_type=jnp.float32,
    )
    local_sum = jnp.sum(gridded * gridded, axis=(2, 3))
    summed = taken_together(local_sum, "wide")
    checksums = collect(summed, "grp", 0) / (LAT * LON)
    return (gridded, checksums)


def solution(mesh):
    placed = (P(None, "grp", "wide", None, None), P("wide", None, None), P(), P())
    return jax.shard_map(
        local,
        mesh=mesh,
        in_specs=placed,
        out_specs=(P("grp", None, "wide", None), P()),
        check_vma=False,
    )
```

profile of v0, /device:TPU:1, one launch (start us, length us, event | category | flops | bytes accessed | tf_op | source)
XLA Modules:
  0.0 446.5 jit_solution(8228078379632217625)
XLA Ops:
  0.6 0.0 copy-start
  0.7 0.9 dynamic-slice_subtract_fusion
  1.6 0.1 iota_compare_fusion
  1.7 0.1 compare_select_fusion.2
  1.8 44.3 %rev.4 = f32[5,641,320]{1,2,0:T(8,128)} reverse(f32[5,641,320]{1,2,0:T(8,128)} %param.5), dimensions={2} | reverse | bytes 8204800 | tf_op jit(solution)/shard_map/jit(_flip)/rev | solution.py:47
  46.1 0.0 copy-start.5
  46.1 7.0 %copy.43 = f32[5,641,320]{2,1,0:T(8,128)} copy(f32[5,641,320]{1,2,0:T(8,128)} %param.5) | data formatting | bytes 8204800 | tf_op args[1]
  53.1 0.0 copy-done.5
  53.1 7.0 %copy.44 = f32[5,641,320]{2,1,0:T(8,128)} copy(f32[5,641,320]{1,2,0:T(8,128)} %rev.4) | data formatting | bytes 8204800 | tf_op jit(solution)/shard_map/jit(_flip)/rev | solution.py:47
  60.1 0.1 maximum_select_fusion
  60.2 0.0 copy-done
  60.2 5.2 %gather_fusion = f32[8,12,5,2,641]{4,3,2,1,0:T(2,128)} fusion(f32[8,12,5,2,641]{4,3,2,1,0:T(2,128)S(1)} %copy-done, s32[1024]{0:T(1024)S(1)} %pad_clamp_fusion), kind=kCustom, calls=%fused_computation | custom fusion | bytes 4922912 | tf_op jit(solution)/shard_map/jit(_take)/gather | solution.py:75
  65.4 0.0 copy-start.2
  65.4 3.3 select_bitcast_fusion
  68.8 0.0 copy-done.2
  68.8 8.9 %broadcast_multiply_fusion = (f32[5,641,2,320]{3,1,2,0:T(8,128)}, f32[5,641,2,320]{3,1,2,0:T(8,128)}) fusion(f32[5,641,320]{2,1,0:T(8,128)S(1)} %copy-done.2, f32[5,641,2]{1,2,0:T(2,128)S(1)} %maximum_select_fusion, f32[5,641,320]{2,1,0:T(8,128)} %copy.43, f32[5,641,2]{1,2,0:T(2,128)S(1)} %fusion.26), kind=kLoop, calls=%fused_computation.10 | loop fusion | flops 4102400 | bytes 24665680 | tf_op jit(solution)/shard_map/mul | solution.py:47
  77.7 21.6 %fusion = f32[5,8,12,2,2,640]{5,2,4,3,1,0:T(8,128)} fusion(f32[5,641,2,320]{3,1,2,0:T(8,128)} %get-tuple-element.10, f32[5,641,2,320]{3,1,2,0:T(8,128)} %get-tuple-element.11, f32[8,12,5,2,641,1]{4,3,2,1,0,5:T(2,128)S(1)} %select_bitcast_fusion), kind=kOutput, calls=%fused_computation.2 | convolution fusion | flops 9456031744 | bytes 23786240 | tf_op jit(solution)/shard_map/dot_general | solution.py:52
  99.3 5.4 %copy.46 = f32[5,8,12,2,2,640]{5,4,3,2,0,1:T(2,128)S(1)} copy(f32[5,8,12,2,2,640]{5,2,4,3,1,0:T(8,128)} %fusion) | data formatting | bytes 9830400 | tf_op jit(solution)/shard_map/dot_general | solution.py:52
  104.8 59.8 %all_to_all.46 = f32[5,8,12,2,2,640]{5,4,3,2,0,1:T(2,128)S(1)} all-to-all(f32[5,8,12,2,2,640]{5,4,3,2,0,1:T(2,128)S(1)} %copy.46), channel_id=1, replica_groups=mesh['grp'=4,'wide'=64] {'grp'}, dimensions={1} | all-to-all | bytes 9830400 | tf_op jit(solution)/shard_map/all_to_all | solution.py:79
  164.6 4.4 copy.47
  169.0 18.1 %copy.48 = f32[5,2,48,2,2,640]{2,4,3,1,0,5:T(2,128)} copy(f32[5,2,48,2,2,640]{5,4,3,2,1,0:T(2,128)} %bitcast.34) | data formatting | bytes 9830400 | tf_op jit(solution)/shard_map/all_to_all | solution.py:79
  187.1 24.2 %reshape.298 = f32[64,1,19200]{2,1,0:T(1,128)} reshape(f32[640,5,2,2,2,48]{5,4,3,2,1,0:T(2,128)} %bitcast.32) | data formatting | bytes 9830400
  211.4 0.0 copy-start.4
  211.4 14.2 %all-to-all-start.1 = ((f32[64,1,19200]{2,1,0:T(1,128)}), f32[64,1,19200]{2,1,0:T(1,128)}, u32[]{:S(2)}, u32[]{:S(2)}) async-start(f32[64,1,19200]{2,1,0:T(1,128)} %reshape.298), calls=%async_computation.1 | async-start | bytes 9830400 | tf_op jit(solution)/shard_map/all_to_all | solution.py:78
  225.6 0.0 copy-done.4
  225.7 16.0 %cosine_multiply_fusion = (f32[320,1,2,1280]{3,0,2,1:T(8,128)}, f32[320,1,2,1280]{3,0,2,1:T(8,128)}) fusion(s32[320,2]{0,1:T(2,128)S(1)} %pad_add_fusion.1, f32[320,2]{0,1:T(2,128)S(1)} %get-tuple-element.4, f32[320,2]{0,1:T(2,128)S(1)} %get-tuple-element.5), kind=kLoop, calls=%fused_computation.19 | loop fusion | flops 9011200 | bytes 6561280 | tf_op jit(solution)/shard_map/mul | solution.py:67
  241.7 95.2 %all-to-all-done.1 = f32[64,1,19200]{2,1,0:T(1,128)} async-done(((f32[64,1,19200]{2,1,0:T(1,128)}), f32[64,1,19200]{2,1,0:T(1,128)}, u32[]{:S(2)}, u32[]{:S(2)}) %all-to-all-start.1) | async-done | bytes 4915232 | tf_op jit(solution)/shard_map/all_to_all | solution.py:78
  337.0 0.5 broadcast.348
  337.5 16.1 %reduce = f32[64,19200]{1,0:T(8,128)} reduce(f32[64,1,19200]{2,1,0:T(1,128)} %all-to-all-done.1, f32[]{:T(128)} %broadcast.348), dimensions={1}, to_apply=%all_to_all.36.reduce_sub_computation | reduce | bytes 9830404 | tf_op jit(solution)/shard_map/all_to_all | solution.py:78
  353.5 23.5 %reshape.299 = f32[640,5,2,2,2,48]{5,4,3,2,1,0:T(2,128)} reshape(f32[64,19200]{1,0:T(8,128)} %reduce) | data formatting | bytes 9830400
  377.0 0.0 copy-start.3
  377.0 6.3 %copy.50 = f32[64,5,2,48,2,2,10]{3,5,6,4,2,1,0:T(2,128)S(1)} copy(f32[64,5,2,48,2,2,10]{3,5,4,2,1,6,0:T(2,128)} %bitcast.31) | data formatting | bytes 9830400 | tf_op jit(solution)/shard_map/all_to_all | solution.py:78
  383.4 0.0 copy-done.3
  383.4 0.0 copy-start.1
  383.4 40.4 %multiply_reduce_fusion = (f32[2,48]{1,0:T(2,128)S(1)}, f32[2,48,10,1280]{3,1,2,0:T(8,128)}) fusion(f32[320,1,2,1280]{3,0,2,1:T(8,128)} %get-tuple-element.3, f32[320,1,2,1280]{3,0,2,1:T(8,128)S(1)} %copy-done.3, f32[320,2,48,2,2,10]{2,4,5,3,1,0:T(2,128)S(1)} %bitcast.35), kind=kOutput, calls=%fused_computation.12 | convolution fusion | flops 18878464000 | bytes 16384384 | tf_op jit(solution)/shard_map/dot_general | solution.py:86
  423.8 15.4 %all_to_all.47 = f32[64,2,48]{2,1,0:T(2,128)S(1)} all-to-all(f32[64,2,48]{2,1,0:T(2,128)S(1)} %broadcast_in_dim.60), channel_id=1, replica_groups=mesh['grp'=4,'wide'=64] {'wide'}, dimensions={0} | all-to-all | bytes 49152 | tf_op jit(solution)/shard_map/all_to_all | solution.py:18
  439.2 0.1 reduce_sum.19
  439.3 6.5 %all_to_all.48 = f32[4,2,48]{2,1,0:T(2,128)S(1)} all-to-all(f32[4,2,48]{2,1,0:T(2,128)S(1)} %broadcast_in_dim.61), channel_id=1, replica_groups=mesh['grp'=4,'wide'=64] {'grp'}, dimensions={0} | all-to-all | bytes 3072 | tf_op jit(solution)/shard_map/all_to_all | solution.py:18
  445.7 0.6 broadcast_multiply_fusion.2
  446.3 0.0 copy-done.1
  (13 shorter events, 0.1 us)
Async XLA Ops:
  0.6 59.6 %copy-start = (f32[8,12,5,2,641]{4,3,2,1,0:T(2,128)S(1)}, f32[8,12,5,2,641]{4,3,2,1,0:T(2,128)}, u32[]{:S(2)}) copy-start(f32[8,12,5,2,641]{4,3,2,1,0:T(2,128)} %param.4) | copy-start | bytes 7384324
  46.1 7.0 %copy-start.5 = (s32[8]{0:T(128)S(1)}, s32[8]{0:T(128)}, u32[]{:S(2)}) copy-start(s32[8]{0:T(128)} %param.7) | copy-start | bytes 100
  65.4 3.3 copy-start.2
  211.4 14.3 %copy-start.4 = (s32[320]{0:T(512)S(1)}, s32[320]{0:T(512)}, u32[]{:S(2)}) copy-start(s32[320]{0:T(512)} %param.6) | copy-start | bytes 3844
  211.4 125.6 %all-to-all-start.1 = ((f32[64,1,19200]{2,1,0:T(1,128)}), f32[64,1,19200]{2,1,0:T(1,128)}, u32[]{:S(2)}, u32[]{:S(2)}) async-start(f32[64,1,19200]{2,1,0:T(1,128)} %reshape.298), calls=%async_computation.1 | async-start | bytes 9830400 | tf_op jit(solution)/shard_map/all_to_all | solution.py:78
  377.0 6.3 %copy-start.3 = (f32[320,1,2,1280]{3,0,2,1:T(8,128)S(1)}, f32[320,1,2,1280]{3,0,2,1:T(8,128)}, u32[]{:S(2)}) copy-start(f32[320,1,2,1280]{3,0,2,1:T(8,128)} %get-tuple-element.2) | copy-start | bytes 9830404
  383.4 63.0 %copy-start.1 = (f32[8,12,5,2,641]{4,3,2,1,0:T(2,128)S(1)}, f32[8,12,5,2,641]{4,3,2,1,0:T(2,128)}, u32[]{:S(2)}) copy-start(f32[8,12,5,2,641]{4,3,2,1,0:T(2,128)} %param.4) | copy-start | bytes 7384324
where the time goes:
time: 453 us; the launch traced here: 447 us
  local copies, waits for them, and re-layouts  146 us (32%)
  waiting for transfers between devices  95.2 us (21%)
  blocking collectives  81.7 us (18%)
  matrix products  62 us (14%)
  other arithmetic  46.3 us (10%)
  starting transfers between devices  14.2 us (3%)
    all_to_all x1, waiting for transfers between devices, local(): lax.all_to_all(lax.all_to_all(fourier, 'grp', split_axis=1, concat_axis=2...  95.2 us
    all_to_all x1, blocking collectives, local(): lax.all_to_all(fourier, 'grp', split_axis=1, concat_axis=2, tiled=True)  59.8 us
    unnamed x15, local copies, waits for them, and re-layouts  54.8 us
    rev x2, local copies, waits for them, and re-layouts, legendre_table(): south = (belong * signs)[..., None] * jnp.flip(legendre, -1)[:, :, None, :]  51.2 us
    dot_general x1, matrix products, local(): lax.dot_general(arrived, synthesis, (((0, 3, 4), (0, 1, 2)), ((), ())), p...  40.4 us
    all_to_all x2, local copies, waits for them, and re-layouts, local(): lax.all_to_all(fourier, 'grp', split_axis=1, concat_axis=2, tiled=True)  22.5 us
    all_to_all x2, blocking collectives, from_everyone(): return lax.all_to_all(copies, axis, split_axis=0, concat_axis=0, tiled=True)  21.9 us
    dot_general x1, matrix products, legendre_sums(): lax.dot_general(coeffs, table, (((4,), (1,)), ((2,), (0,))), precision=HI...  21.6 us
  transfers between devices with their start and end apart: 1, of which 1 were waited for; matrix products, arithmetic and copies ran while one was open for 4% of the time, Pallas kernels for 0%

commit v1 on v0

v1 whole, which is shorter than its diff:
```python
import functools
import math

import jax
import jax.numpy as jnp
from jax import lax
from jax.experimental import pallas as pl
from jax.experimental.pallas import tpu as pltpu
from jax.sharding import PartitionSpec as P

WAVES = 640
LAT = 640
LON = 1280
HALF = LON // 2
MESH = pl.DeviceIdType.MESH
ROWS = 40
LAST = 32
GROUPS = 4
PEERS = 64


def split(value):
    high = value.astype(jnp.bfloat16)
    low = (value - high.astype(jnp.float32)).astype(jnp.bfloat16)
    return high, low


def kernel(
    pair,
    fields,
    spectral,
    table_hbm,
    table_end,
    pairs_down,
    out,
    sums_out,
    table,
    table_high,
    table_low,
    coeffs_send,
    coeffs,
    waves_send,
    last_send,
    waves,
    last,
    synth_high,
    synth_low,
    left_high,
    left_low,
    energy,
    sums,
    table_sem,
    coeffs_send_sem,
    coeffs_sem,
    waves_send_sem,
    waves_sem,
    sums_send_sem,
    sums_sem,
):
    grp = lax.axis_index("grp")
    wide = lax.axis_index("wide")
    my_y, my_z, my_c = wide // 16, (wide // 2) % 8, wide % 2
    south = wide // 32

    def other_group(step):
        return lax.rem(grp + step, GROUPS)

    def partner(i):
        k = i % 8
        up = (k + 2) // 2
        dz = (k % 2) * (8 - up) + (1 - k % 2) * up
        dz = (1 - k // 6) * dz + (k // 6) * (1 - k % 2) * 4
        dy = 3 - (i // 8) % 4
        dc = 1 - i // 32
        return (
            lax.rem(my_y + dy, 4) * 16 + lax.rem(my_z + dz, 8) * 2 + lax.rem(my_c + dc, 2)
        )

    def block_of(dest):
        return dest + (dest // 32) * (95 - 2 * dest)

    barrier = pltpu.get_barrier_semaphore()
    table_copies = [
        pltpu.make_async_copy(
            table_hbm.at[:, :, tile * 128 : (tile + 1) * 128],
            table.at[tile],
            table_sem.at[tile],
        )
        for tile in range(5)
    ] + [pltpu.make_async_copy(table_end, table.at[5], table_sem.at[5])]
    for copy in table_copies:
        copy.start()

    def greet(i, carry):
        pl.semaphore_signal(
            barrier, inc=1, device_id={"grp": grp, "wide": partner(i)}, device_id_type=MESH
        )
        return carry

    lax.fori_loop(0, PEERS - 1, greet, 0)
    for step in (1, 2, 3):
        pl.semaphore_signal(
            barrier,
            inc=1,
            device_id={"grp": other_group(step), "wide": wide},
            device_id_type=MESH,
        )

    coeffs_send[:, :, :, 640:768] = jnp.zeros((GROUPS, 15, 16, 128), jnp.float32)

    for slot in range(5):

        def reorder(group, carry, slot=slot):
            for j in range(2):
                field = fields[2 * group + j]
                for level in range(12):
                    q, l = level // 4, level % 4
                    block = q * 4 + slot if slot < 4 else 12 + q
                    for c in range(2):
                        coeffs_send[group, block, c * 8 + j * 4 + l, 0:641] = spectral[
                            field, level, slot, c, :
                        ]
            return carry

        lax.fori_loop(0, GROUPS, reorder, 0)

    pl.semaphore_wait(barrier, PEERS - 1 + GROUPS - 1)

    def coeffs_copy(chunk, step):
        blocks = pl.ds(chunk * 4, 4 if chunk < 3 else 3)
        dest = other_group(step)
        return pltpu.make_async_remote_copy(
            src_ref=coeffs_send.at[dest, blocks],
            dst_ref=coeffs.at[grp, blocks],
            send_sem=coeffs_send_sem.at[chunk],
            recv_sem=coeffs_sem.at[chunk],
            device_id={"grp": dest, "wide": wide},
            device_id_type=MESH,
        )

    def coeffs_all(chunk):
        blocks = pl.ds(chunk * 4, 4 if chunk < 3 else 3)
        return pltpu.make_async_remote_copy(
            src_ref=coeffs_send.at[0:3, blocks],
            dst_ref=coeffs.at[0:3, blocks],
            send_sem=coeffs_send_sem.at[chunk],
            recv_sem=coeffs_sem.at[chunk],
            device_id={"grp": other_group(1), "wide": wide},
            device_id_type=MESH,
        )

    for chunk in (0, 1, 3, 2):
        for step in (1, 2, 3):
            coeffs_copy(chunk, step).start()

    def keep_own(block, carry):
        coeffs[grp, block] = coeffs_send[grp, block]
        return carry

    lax.fori_loop(0, 15, keep_own, 0)

    for copy in table_copies:
        copy.wait()

    def part_table(i, carry):
        slot, lat = i // 10, i % 10
        rows = pl.ds(pl.multiple_of(lat * 32, 32), 32)
        for tile in range(6):
            value = table[tile, slot, pl.ds(lat, 32, stride=10), :]
            high, low = split(value)
            table_high[slot, rows, tile * 128 : (tile + 1) * 128] = high
            table_low[slot, rows, tile * 128 : (tile + 1) * 128] = low
        return carry

    lax.fori_loop(0, 50, part_table, 0)

    energy[...] = jnp.zeros_like(energy)
    degree = lax.broadcasted_iota(jnp.int32, (1, 768), 1)
    lane = lax.broadcasted_iota(jnp.int32, (1, 128), 1)

    def legendre(block, slot, q, target, first_row, stride):
        p = pair[wide * 5 + slot]
        boundary = WAVES - p
        first_part = degree < boundary
        start = jnp.where(first_part, 0, boundary)
        sign = 1.0 - 2.0 * ((degree - start) % 2).astype(jnp.float32)
        is_first = first_part.astype(jnp.float32)
        inside = (degree <= WAVES).astype(jnp.float32)
        odd = (p % 2).astype(jnp.float32)
        even_mask = (is_first * (1.0 - odd) + (1.0 - is_first) * odd) * inside
        odd_mask = (1.0 - even_mask) * inside
        x = jnp.concatenate([coeffs[g, block] for g in range(GROUPS)], 0)
        right = jnp.concatenate(
            [x * even_mask, x * odd_mask, x * (even_mask * sign), x * (odd_mask * sign)], 0
        )
        right_high, right_low = split(right)
        nt = (((1,), (1,)), ((), ()))

        def dot(a, b):
            return lax.dot_general(a, b, nt, preferred_element_type=jnp.float32)

        left = table_high[slot]
        result = dot(left, right_high) + dot(left, right_low) + dot(table_low[slot], right_high)
        for lat in range(10):
            rows = result[lat * 32 : (lat + 1) * 32]
            target[pl.ds(first_row + lat, 32, stride=stride), :] = rows[:, 0:128]
            target[pl.ds(first_row + lat + 32 * stride, 32, stride=stride), :] = rows[:, 128:256]
        squares = result * result
        squares = squares[:, 0:128] + squares[:, 128:256]
        total = jnp.sum(squares.reshape(40, 8, 128), axis=0)
        real = 1.0 - ((lane // 8) % 2).astype(jnp.float32)
        zero = jnp.where(p == 0, 1.0, 0.0) * jnp.where(lane < 64, 1.0, 0.0)
        energy[q] = energy[q] + total * (2.0 * (1.0 - zero) + real * zero)

    def wave_copy(chunk, i):
        dest = partner(i)
        size = ROWS if chunk < 3 else LAST
        source = waves_send.at[chunk] if chunk < 3 else last_send
        sink = waves.at[chunk] if chunk < 3 else last
        return pltpu.make_async_remote_copy(
            src_ref=source.at[pl.ds(pl.multiple_of(block_of(dest) * size, 8), size)],
            dst_ref=sink.at[pl.ds(pl.multiple_of(wide * size, 8), size)],
            send_sem=waves_send_sem.at[chunk],
            recv_sem=waves_sem.at[chunk],
            device_id={"grp": grp, "wide": dest},
            device_id_type=MESH,
        )

    def wave_all(chunk):
        size = ROWS if chunk < 3 else LAST
        source = waves_send.at[chunk] if chunk < 3 else last_send
        sink = waves.at[chunk] if chunk < 3 else last
        return pltpu.make_async_remote_copy(
            src_ref=source.at[pl.ds(0, (PEERS - 1) * size)],
            dst_ref=sink.at[pl.ds(0, (PEERS - 1) * size)],
            send_sem=waves_send_sem.at[chunk],
            recv_sem=waves_sem.at[chunk],
            device_id={"grp": grp, "wide": partner(0)},
            device_id_type=MESH,
        )

    def send_waves(chunk):
        def one(i, carry):
            wave_copy(chunk, i).start()
            return carry

        lax.fori_loop(0, PEERS - 1, one, 0)
        size = ROWS if chunk < 3 else LAST
        source = waves_send.at[chunk] if chunk < 3 else last_send
        sink = waves.at[chunk] if chunk < 3 else last
        sink[pl.ds(pl.multiple_of(wide * size, 8), size), :] = source[
            pl.ds(pl.multiple_of(block_of(wide) * size, 8), size), :
        ]

    def legendre_chunk(q):
        coeffs_all(q).wait_recv()

        def one(slot, carry):
            legendre(q * 4 + slot, slot, q, waves_send.at[q], slot * 10, ROWS)
            return carry

        lax.fori_loop(0, 4, one, 0)

    legendre_chunk(0)
    send_waves(0)
    legendre_chunk(1)
    send_waves(1)
    coeffs_all(3).wait_recv()

    def last_slot(q, carry):
        legendre(12 + q, 4, q, last_send, q * 10, LAST)
        return carry

    lax.fori_loop(0, 3, last_slot, 0)
    legendre_chunk(2)

    def folded(q):
        row = jnp.sum(energy[q], axis=0, keepdims=True)
        row = row + pltpu.roll(row, 64, 1)
        low_part = (lane // 8) % 2 == 0
        return row + jnp.where(low_part, pltpu.roll(row, 120, 1), pltpu.roll(row, 8, 1))

    shares = jnp.where(
        lane < 64, jnp.where((lane // 8) % 2 == 0, folded(0), folded(1)), folded(2)
    )
    shares = jnp.broadcast_to(shares, (64, 128))
    last_send[pl.ds(30, 64, stride=LAST), :] = shares
    last_send[pl.ds(31, 64, stride=LAST), :] = shares
    send_waves(3)
    send_waves(2)

    def cosine(phase):
        phase = phase - LON * jnp.floor(phase * (1.0 / LON) + 0.5)
        angle = (LON // 4 - jnp.abs(phase)) * (2.0 * math.pi / LON)
        square = angle * angle
        series = 1.0 / 6227020800.0
        for term in (-1.0 / 39916800.0, 1.0 / 362880.0, -1.0 / 5040.0, 1.0 / 120.0, -1.0 / 6.0, 1.0):
            series = series * square + term
        return series * angle

    column = lax.broadcasted_iota(jnp.int32, (64, 128), 1)

    def make_synthesis(i, carry):
        parity, slot = i // 5, i % 5
        p = pairs_down[pl.ds(pl.multiple_of(slot * 64, 64), 64), :]
        number = jnp.where(p % 2 == parity, p, WAVES - 1 - p)
        factor = jnp.where(number == 0, 1.0, 2.0)
        cos_row = pl.multiple_of(slot * 64 + (slot // 4) * 256, 64)
        sin_row = pl.multiple_of(256 + slot * 64 + (slot // 4) * 64, 64)
        for tile in range(5):
            phase = (number * (column + tile * 128)).astype(jnp.float32)
            lanes = pl.ds(tile * 128, 128)
            high, low = split(factor * cosine(phase))
            synth_high[parity, pl.ds(cos_row, 64), lanes] = high
            synth_low[parity, pl.ds(cos_row, 64), lanes] = low
            high, low = split(-factor * cosine(phase - LON // 4))
            synth_high[parity, pl.ds(sin_row, 64), lanes] = high
            synth_low[parity, pl.ds(sin_row, 64), lanes] = low
        return carry

    lax.fori_loop(0, 10, make_synthesis, 0)

    def synthesis(q):
        def turn(lat, carry):
            main = jnp.concatenate(
                [waves[q, pl.ds(s * 10 + lat, 64, stride=ROWS), :] for s in range(4)], 0
            )
            main = main.T.reshape(2, 4, 2, 8, 256)
            rest = last[pl.ds(q * 10 + lat, 64, stride=LAST), :].T.reshape(2, 4, 2, 8, 64)
            rows = pl.ds(pl.multiple_of(lat * 32, 32), 32)
            for parity in range(2):
                for c in range(2):
                    high, low = split(main[parity, :, c].reshape(32, 256))
                    left_high[parity, rows, c * 256 : (c + 1) * 256] = high
                    left_low[parity, rows, c * 256 : (c + 1) * 256] = low
                high, low = split(
                    jnp.concatenate(
                        [rest[parity, :, 0].reshape(32, 64), rest[parity, :, 1].reshape(32, 64)], 1
                    )
                )
                left_high[parity, rows, 512:640] = high
                left_low[parity, rows, 512:640] = low
            return carry

        lax.fori_loop(0, 10, turn, 0)

        def dot(a, b):
            return jnp.dot(a, b, preferred_element_type=jnp.float32)

        for start, width in ((0, 256), (256, 256), (512, 128)):
            halves = []
            for parity in range(2):
                right_high = synth_high[parity, :, start : start + width]
                right_low = synth_low[parity, :, start : start + width]
                halves.append(
                    dot(left_high[parity], right_high)
                    + dot(left_high[parity], right_low)
                    + dot(left_low[parity], right_high)
                )
            for value, offset in ((halves[0] + halves[1], 0), (halves[0] - halves[1], HALF)):
                for lat in range(10):
                    place = lat + south * (9 - 2 * lat)
                    for g in range(GROUPS):
                        for j in range(2):
                            row = lat * 32 + g * 8 + j * 4
                            level = g * 12 + q * 4
                            out[
                                j,
                                place,
                                level : level + 4,
                                offset + start : offset + start + width,
                            ] = value[row : row + 4]

    wave_all(0).wait_recv()
    wave_all(1).wait_recv()
    wave_all(3).wait_recv()

    total = jnp.sum(last[pl.ds(30, 64, stride=LAST), :], axis=0, keepdims=True)
    sums[grp] = jnp.broadcast_to(total, (8, 128))

    def sums_copy(step):
        dest = other_group(step)
        return pltpu.make_async_remote_copy(
            src_ref=sums.at[grp],
            dst_ref=sums.at[grp],
            send_sem=sums_send_sem,
            recv_sem=sums_sem,
            device_id={"grp": dest, "wide": wide},
            device_id_type=MESH,
        )

    synthesis(0)
    for step in (1, 2, 3):
        sums_copy(step).start()
    synthesis(1)
    sums_all = pltpu.make_async_remote_copy(
        src_ref=sums.at[0:3],
        dst_ref=sums.at[0:3],
        send_sem=sums_send_sem,
        recv_sem=sums_sem,
        device_id={"grp": other_group(1), "wide": wide},
        device_id_type=MESH,
    )
    sums_all.wait_send()
    sums_all.wait_recv()
    sums_out[...] = sums[...]
    wave_all(2).wait_recv()
    synthesis(2)
    for chunk in range(4):
        coeffs_all(chunk).wait_send()
        wave_all(chunk).wait_send()


def local(spectral, legendre, pair_table, field_map):
    table = jnp.swapaxes(legendre, 1, 2)
    table_end = jnp.pad(table[:, :, 640:641], ((0, 0), (0, 0), (0, 127)))
    by_slot = pair_table.reshape(PEERS, 5).T.reshape(-1, 1)
    pairs_down = jnp.broadcast_to(by_slot, (320, 128))
    smem = pl.BlockSpec(memory_space=pltpu.SMEM)
    vmem = pl.BlockSpec(memory_space=pltpu.VMEM)
    anywhere = pl.BlockSpec(memory_space=pl.ANY)
    dma = pltpu.SemaphoreType.DMA
    grid, sums = pl.pallas_call(
        kernel,
        name="transform",
        out_shape=(
            jax.ShapeDtypeStruct((2, 10, 48, LON), jnp.float32),
            jax.ShapeDtypeStruct((GROUPS, 8, 128), jnp.float32),
        ),
        in_specs=[smem, smem, vmem, anywhere, anywhere, vmem],
        out_specs=(vmem, vmem),
        scratch_shapes=[
            pltpu.VMEM((6, 5, 320, 128), jnp.float32),
            pltpu.VMEM((5, 320, 768), jnp.bfloat16),
            pltpu.VMEM((5, 320, 768), jnp.bfloat16),
            pltpu.VMEM((GROUPS, 15, 16, 768), jnp.float32),
            pltpu.VMEM((GROUPS, 15, 16, 768), jnp.float32),
            pltpu.VMEM((3, PEERS * ROWS, 128), jnp.float32),
            pltpu.VMEM((PEERS * LAST, 128), jnp.float32),
            pltpu.VMEM((3, PEERS * ROWS, 128), jnp.float32),
            pltpu.VMEM((PEERS * LAST, 128), jnp.float32),
            pltpu.VMEM((2, HALF, HALF), jnp.bfloat16),
            pltpu.VMEM((2, HALF, HALF), jnp.bfloat16),
            pltpu.VMEM((2, 320, HALF), jnp.bfloat16),
            pltpu.VMEM((2, 320, HALF), jnp.bfloat16),
            pltpu.VMEM((3, 8, 128), jnp.float32),
            pltpu.VMEM((GROUPS, 8, 128), jnp.float32),
            dma((6,)),
            dma((4,)),
            dma((4,)),
            dma((4,)),
            dma((4,)),
            dma,
            dma,
        ],
        compiler_params=pltpu.CompilerParams(
            collective_id=0, has_side_effects=True, vmem_limit_bytes=58 * 2**20
        ),
    )(pair_table, field_map, spectral, table, table_end, pairs_down)
    grid = jnp.swapaxes(grid, 1, 2)
    by_part = sums[:, 0, :].reshape(GROUPS, 2, 4, 2, 2, 4)
    chunks = jnp.stack([by_part[:, 0, :, 0], by_part[:, 0, :, 1], by_part[:, 1, :, 0]], 1)
    checksums = jnp.transpose(chunks, (0, 3, 2, 1, 4)).reshape(8, 48) * (1.0 / LAT)
    return grid, checksums


def solution(mesh):
    placed = (P(None, "grp", "wide", None, None), P("wide", None, None), P(), P())
    return jax.shard_map(
        local,
        mesh=mesh,
        in_specs=placed,
        out_specs=(P("grp", None, "wide", None), P()),
        check_vma=False,
    )
```

time: 453 us -> 154 us (0.34); the launches traced: 447 us -> 152 us
  Pallas kernels: 0 us -> 141 us
  local copies, waits for them, and re-layouts: 146 us -> 10.5 us
  waiting for transfers between devices: 95.2 us -> 0 us
  blocking collectives: 81.7 us -> 0 us
  matrix products: 62 us -> 0 us
  other arithmetic: 46.3 us -> 0.04 us
  starting transfers between devices: 14.2 us -> 0 us
    pallas_call x0 -> x1, Pallas kernels: none -> 141 us  [local(): pl.pallas_call(kernel, name='transform', out_shape=(jax.ShapeDtypeStruct(...]
    all_to_all x1 -> x0, waiting for transfers between devices: 95.2 us -> none  [local(): lax.all_to_all(lax.all_to_all(fourier, 'grp', split_axis=1, concat_axis=2...]
    all_to_all x3 -> x0, blocking collectives: 81.7 us -> none  [the longest x1 59.8 us: local(): lax.all_to_all(fourier, 'grp', split_axis=1, concat_axis=2, tiled=True)]
    dot_general x2 -> x0, matrix products: 62 us -> none  [the longest x1 40.4 us: local(): lax.dot_general(arrived, synthesis, (((0, 3, 4), (0, 1, 2)), ((), ())), p...]
    rev x2 -> x0, local copies, waits for them, and re-layouts: 51.2 us -> none  [legendre_table(): south = (belong * signs)[..., None] * jnp.flip(legendre, -1)[:, :, None, :]]
    unnamed x15 -> x1, local copies, waits for them, and re-layouts: 54.8 us -> 5 us
    all_to_all x4 -> x0, local copies, waits for them, and re-layouts: 29.4 us -> none  [the longest x2 22.5 us: local(): lax.all_to_all(fourier, 'grp', split_axis=1, concat_axis=2, tiled=True)]
    mul x3 -> x1, other arithmetic: 25 us -> 0.04 us  [local(): jnp.transpose(chunks, (0, 3, 2, 1, 4)).reshape(8, 48) * (1.0 / LAT)]
  transfers between devices with their start and end apart: 1 -> 0, of which waited for: 1 -> 0; matrix products, arithmetic and copies ran while one was open for 4% -> 0% of each run, Pallas kernels for 0% -> 0%
where the time goes in v1:
time: 154 us; the launch traced here: 152 us
  Pallas kernels  141 us (92%)
  local copies, waits for them, and re-layouts  10.5 us (7%)
    pallas_call x1, Pallas kernels, local(): pl.pallas_call(kernel, name='transform', out_shape=(jax.ShapeDtypeStruct(...  141 us
    unnamed x1, local copies, waits for them, and re-layouts  5 us

profile of v1, /device:TPU:1, one launch (start us, length us, event | category | flops | bytes accessed | tf_op | source)
XLA Modules:
  0.0 152.1 jit_solution(18079884432506942394)
XLA Ops:
  0.6 1.2 slice.20
  1.8 1.0 pad.4.table_end
  2.8 0.8 reshape.12
  3.6 0.1 copy.9
  3.7 0.1 broadcast_in_dim.7
  3.8 0.8 broadcast_in_dim.8.pairs_down
  4.5 140.8 %transform.1 = (f32[2,10,48,1280]{3,2,1,0:T(8,128)}, f32[4,8,128]{2,1,0:T(8,128)}) custom-call(s32[320]{0:T(512)} %pair.1, s32[8]{0:T(128)} %fields.1, f32[8,12,5,2,641]{4,3,2,1,0:T(2,128)} %spectral.1, f32[5,320,641]{2,1,0:T(8,128)} %bitcast.18, f32[5,320,128]{2,1,0:T(8,128)} %pad.4.table_end, s32[320,128]{1,0:T(8,128)} %broadcast_in_dim.8.pairs_down), custom_call_target="tpu_custom_call" | custom-call | tf_op jit(solution)/shard_map/transform/pallas_call | solution.py:423
  145.4 0.7 slice_reduce_fusion
  146.1 0.1 reshape_squeeze.3
  146.4 0.7 mul.15
  147.1 5.0 %copy.18 = f32[2,48,10,1280]{3,1,2,0:T(8,128)} copy(f32[2,48,10,1280]{3,1,2,0:T(8,128)} %bitcast.19) | data formatting | bytes 9830400
  (3 shorter events, 0.1 us)

commit v2 on v1

--- a/solution.py
+++ b/solution.py
@@ -30,11 +30,11 @@
     fields,
     spectral,
     table_hbm,
-    table_end,
-    pairs_down,
     out,
     sums_out,
+    table_whole,
     table,
+    pairs_down,
     table_high,
     table_low,
     coeffs_send,
@@ -47,13 +47,18 @@
     synth_low,
     left_high,
     left_low,
+    left,
     energy,
+    shares_send,
+    shares,
     sums,
     table_sem,
     coeffs_send_sem,
     coeffs_sem,
     waves_send_sem,
     waves_sem,
+    shares_send_sem,
+    shares_sem,
     sums_send_sem,
     sums_sem,
 ):
@@ -87,7 +92,7 @@
             table_sem.at[tile],
         )
         for tile in range(5)
-    ] + [pltpu.make_async_copy(table_end, table.at[5], table_sem.at[5])]
+    ] + [pltpu.make_async_copy(table_hbm, table_whole, table_sem.at[5])]
     for copy in table_copies:
         copy.start()
 
@@ -108,26 +113,22 @@
 
     coeffs_send[:, :, :, 640:768] = jnp.zeros((GROUPS, 15, 16, 128), jnp.float32)
 
-    for slot in range(5):
-
-        def reorder(group, carry, slot=slot):
-            for j in range(2):
-                field = fields[2 * group + j]
-                for level in range(12):
-                    q, l = level // 4, level % 4
-                    block = q * 4 + slot if slot < 4 else 12 + q
-                    for c in range(2):
-                        coeffs_send[group, block, c * 8 + j * 4 + l, 0:641] = spectral[
-                            field, level, slot, c, :
-                        ]
-            return carry
-
-        lax.fori_loop(0, GROUPS, reorder, 0)
-
-    pl.semaphore_wait(barrier, PEERS - 1 + GROUPS - 1)
+    def reorder(i, carry):
+        group, slot = lax.rem(grp + i // 5, GROUPS), i % 5
+        for j in range(2):
+            field = fields[2 * group + j]
+            for level in range(12):
+                q, l = level // 4, level % 4
+                for c in range(2):
+                    coeffs_send[group, q * 5 + slot, c * 8 + j * 4 + l, 0:641] = spectral[
+                        field, level, slot, c, :
+                    ]
+        return carry
+
+    lax.fori_loop(0, 5, reorder, 0)
 
     def coeffs_copy(chunk, step):
-        blocks = pl.ds(chunk * 4, 4 if chunk < 3 else 3)
+        blocks = pl.ds(chunk * 5, 5)
         dest = other_group(step)
         return pltpu.make_async_remote_copy(
             src_ref=coeffs_send.at[dest, blocks],
@@ -139,7 +140,7 @@
         )
 
     def coeffs_all(chunk):
-        blocks = pl.ds(chunk * 4, 4 if chunk < 3 else 3)
+        blocks = pl.ds(chunk * 5, 5)
         return pltpu.make_async_remote_copy(
             src_ref=coeffs_send.at[0:3, blocks],
             dst_ref=coeffs.at[0:3, blocks],
@@ -149,18 +150,15 @@
             device_id_type=MESH,
         )
 
-    for chunk in (0, 1, 3, 2):
-        for step in (1, 2, 3):
-            coeffs_copy(chunk, step).start()
-
-    def keep_own(block, carry):
-        coeffs[grp, block] = coeffs_send[grp, block]
-        return carry
-
-    lax.fori_loop(0, 15, keep_own, 0)
-
     for copy in table_copies:
         copy.wait()
+    first_lane = lax.broadcasted_iota(jnp.int32, (320, 128), 1) == 0
+
+    def part_end(slot, carry):
+        table[5, slot] = jnp.where(first_lane, table_whole[slot, :, 640:641], 0.0)
+        return carry
+
+    lax.fori_loop(0, 5, part_end, 0)
 
     def part_table(i, carry):
         slot, lat = i // 10, i % 10
@@ -178,7 +176,7 @@
     degree = lax.broadcasted_iota(jnp.int32, (1, 768), 1)
     lane = lax.broadcasted_iota(jnp.int32, (1, 128), 1)
 
-    def legendre(block, slot, q, target, first_row, stride):
+    def masks(slot):
         p = pair[wide * 5 + slot]
         boundary = WAVES - p
         first_part = degree < boundary
@@ -189,18 +187,41 @@
         odd = (p % 2).astype(jnp.float32)
         even_mask = (is_first * (1.0 - odd) + (1.0 - is_first) * odd) * inside
         odd_mask = (1.0 - even_mask) * inside
-        x = jnp.concatenate([coeffs[g, block] for g in range(GROUPS)], 0)
-        right = jnp.concatenate(
-            [x * even_mask, x * odd_mask, x * (even_mask * sign), x * (odd_mask * sign)], 0
-        )
-        right_high, right_low = split(right)
-        nt = (((1,), (1,)), ((), ()))
-
-        def dot(a, b):
-            return lax.dot_general(a, b, nt, preferred_element_type=jnp.float32)
-
-        left = table_high[slot]
-        result = dot(left, right_high) + dot(left, right_low) + dot(table_low[slot], right_high)
+        return p, even_mask, odd_mask, sign
+
+    def piece(dx, q, slot):
+        if dx is None:
+            return coeffs_send[grp, q * 5 + slot]
+        return coeffs[lax.rem(grp + dx, GROUPS), q * 5 + slot]
+
+    nt = (((1,), (1,)), ((), ()))
+
+    def dot_nt(a, b):
+        return lax.dot_general(a, b, nt, preferred_element_type=jnp.float32)
+
+    def wave_row(slots, members, tiles, groups, target, first_row, stride):
+        result = None
+        zero = jnp.zeros((1, 128), jnp.float32)
+        empty = jnp.zeros((32, 768), jnp.float32)
+        for number, slot in enumerate(slots):
+            p, even_mask, odd_mask, sign = masks(slot)
+            north, southern = [], []
+            for i in range(4):
+                if members[i] == number:
+                    parts = jnp.concatenate([tiles[i] * even_mask, tiles[i] * odd_mask], 0)
+                    north.append(parts)
+                    southern.append(parts * sign)
+                    here = (lane // 32 == i) & (lane % 32 < 16)
+                    zero = zero + jnp.where(p == 0, 1.0, 0.0) * here.astype(jnp.float32)
+                else:
+                    north.append(empty)
+                    southern.append(empty)
+            right_high, right_low = split(jnp.concatenate(north + southern, 0))
+            high = table_high[slot]
+            product = (
+                dot_nt(high, right_high) + dot_nt(high, right_low) + dot_nt(table_low[slot], right_high)
+            )
+            result = product if result is None else result + product
         for lat in range(10):
             rows = result[lat * 32 : (lat + 1) * 32]
             target[pl.ds(first_row + lat, 32, stride=stride), :] = rows[:, 0:128]
@@ -209,8 +230,9 @@
         squares = squares[:, 0:128] + squares[:, 128:256]
         total = jnp.sum(squares.reshape(40, 8, 128), axis=0)
         real = 1.0 - ((lane // 8) % 2).astype(jnp.float32)
-        zero = jnp.where(p == 0, 1.0, 0.0) * jnp.where(lane < 64, 1.0, 0.0)
-        energy[q] = energy[q] + total * (2.0 * (1.0 - zero) + real * zero)
+        total = total * (2.0 * (1.0 - zero) + real * zero)
+        for i in range(4):
+            energy[groups[i]] = energy[groups[i]] + total * (lane // 32 == i).astype(jnp.float32)
 
     def wave_copy(chunk, i):
         dest = partner(i)
@@ -252,41 +274,96 @@
             pl.ds(pl.multiple_of(block_of(wide) * size, 8), size), :
         ]
 
-    def legendre_chunk(q):
+    def own_row(r, carry):
+        wave_row(
+            (r, 4),
+            (0, 0, 0, 1),
+            [piece(None, q, r) for q in range(3)] + [piece(None, r, 4)],
+            (0, 1, 2, r),
+            last_send,
+            r * 10,
+            LAST,
+        )
+        return carry
+
+    lax.fori_loop(0, 2, own_row, 0)
+    wave_row(
+        (2, 3),
+        (0, 0, 1, 1),
+        [piece(None, 0, 2), piece(None, 1, 2), piece(None, 0, 3), piece(None, 1, 3)],
+        (0, 1, 0, 1),
+        last_send,
+        20,
+        LAST,
+    )
+    spare = jnp.zeros((64, 128), jnp.float32)
+    last_send[pl.ds(30, 64, stride=LAST), :] = spare
+    last_send[pl.ds(31, 64, stride=LAST), :] = spare
+
+    pl.semaphore_wait(barrier, PEERS - 1 + GROUPS - 1)
+    send_waves(3)
+    lax.fori_loop(5, 20, reorder, 0)
+    for chunk in range(3):
+        for step in (1, 2, 3):
+            coeffs_copy(chunk, step).start()
+
+    def waves_of(q):
         coeffs_all(q).wait_recv()
-
-        def one(slot, carry):
-            legendre(q * 4 + slot, slot, q, waves_send.at[q], slot * 10, ROWS)
+        e, f, h = (4, 3, 3) if q == 0 else (4, 3, 2) if q == 1 else (3, 4, 4)
+
+        def one(r, carry):
+            wave_row(
+                (r, e),
+                (0, 0, 0, 1),
+                [piece(dx, q, r) for dx in (1, 2, 3)] + [piece(r + 1, q, e)],
+                (3 + q, 6 + q, 9 + q, 3 * (r + 1) + q),
+                waves_send.at[q],
+                r * 10,
+                ROWS,
+            )
             return carry
 
-        lax.fori_loop(0, 4, one, 0)
-
-    legendre_chunk(0)
+        lax.fori_loop(0, 3, one, 0)
+        wave_row(
+            (f,) if f == h else (f, h),
+            (0, 0, 0, 0) if f == h else (0, 0, 0, 1),
+            [piece(dx, q, f) for dx in (1, 2, 3)] + [piece(None, 2, h)],
+            (3 + q, 6 + q, 9 + q, 2),
+            waves_send.at[q],
+            30,
+            ROWS,
+        )
+
+    waves_of(0)
     send_waves(0)
-    legendre_chunk(1)
+    waves_of(1)
     send_waves(1)
-    coeffs_all(3).wait_recv()
-
-    def last_slot(q, carry):
-        legendre(12 + q, 4, q, last_send, q * 10, LAST)
-        return carry
-
-    lax.fori_loop(0, 3, last_slot, 0)
-    legendre_chunk(2)
-
-    def folded(q):
-        row = jnp.sum(energy[q], axis=0, keepdims=True)
-        row = row + pltpu.roll(row, 64, 1)
-        low_part = (lane // 8) % 2 == 0
-        return row + jnp.where(low_part, pltpu.roll(row, 120, 1), pltpu.roll(row, 8, 1))
-
-    shares = jnp.where(
-        lane < 64, jnp.where((lane // 8) % 2 == 0, folded(0), folded(1)), folded(2)
-    )
-    shares = jnp.broadcast_to(shares, (64, 128))
-    last_send[pl.ds(30, 64, stride=LAST), :] = shares
-    last_send[pl.ds(31, 64, stride=LAST), :] = shares
-    send_waves(3)
+    waves_of(2)
+
+    share = jnp.zeros((1, 128), jnp.float32)
+    for group in range(12):
+        row = jnp.sum(energy[group], axis=0, keepdims=True)
+        for shift in (64, 32, 16, 8):
+            row = row + pltpu.roll(row, shift, 1)
+        share = jnp.where(lane // 8 == group, row, share)
+    shares_send[0] = share
+    shares[wide] = share
+
+    def share_copy(i):
+        return pltpu.make_async_remote_copy(
+            src_ref=shares_send.at[0],
+            dst_ref=shares.at[wide],
+            send_sem=shares_send_sem,
+            recv_sem=shares_sem,
+            device_id={"grp": grp, "wide": partner(i)},
+            device_id_type=MESH,
+        )
+
+    def send_share(i, carry):
+        share_copy(i).start()
+        return carry
+
+    lax.fori_loop(0, PEERS - 1, send_share, 0)
     send_waves(2)
 
     def cosine(phase):
@@ -299,6 +376,13 @@
         return series * angle
 
     column = lax.broadcasted_iota(jnp.int32, (64, 128), 1)
+
+    def spread_pairs(i, carry):
+        for slot in range(5):
+            pairs_down[pl.ds(slot * 64 + i, 1), :] = jnp.full((1, 128), pair[i * 5 + slot])
+        return carry
+
+    lax.fori_loop(0, PEERS, spread_pairs, 0)
 
     def make_synthesis(i, carry):
         parity, slot = i // 5, i % 5
@@ -320,29 +404,50 @@
 
     lax.fori_loop(0, 10, make_synthesis, 0)
 
+    def place_of(q, dx, slot):
+        if dx == 0 and q < 2:
+            return {0: (3, 0, q), 1: (3, 1, q), 2: (3, 2, q), 3: (3, 2, 2 + q), 4: (3, q, 3)}[slot]
+        if dx == 0:
+            return {0: (3, 0, 2), 1: (3, 1, 2), 2: (1, 3, 3), 3: (0, 3, 3), 4: (2, 3, 3)}[slot]
+        e, f = (4, 3) if q < 2 else (3, 4)
+        if slot == e:
+            return (q, dx - 1, 3)
+        return (q, 3 if slot == f else slot, dx - 1)
+
     def synthesis(q):
         def turn(lat, carry):
-            main = jnp.concatenate(
-                [waves[q, pl.ds(s * 10 + lat, 64, stride=ROWS), :] for s in range(4)], 0
-            )
-            main = main.T.reshape(2, 4, 2, 8, 256)
-            rest = last[pl.ds(q * 10 + lat, 64, stride=LAST), :].T.reshape(2, 4, 2, 8, 64)
-            rows = pl.ds(pl.multiple_of(lat * 32, 32), 32)
+            turned = {}
+            for dx in range(GROUPS):
+                group = lax.rem(grp + dx, GROUPS)
+                rows = pl.ds(pl.multiple_of(lat * 32 + group * 8, 8), 8)
+                for slot in range(5):
+                    message, row, place = place_of(q, dx, slot)
+                    if (message, row) not in turned:
+                        if message < 3:
+                            value = waves[message, pl.ds(row * 10 + lat, 64, stride=ROWS), :]
+                        else:
+                            value = last[pl.ds(row * 10 + lat, 64, stride=LAST), :]
+                        turned[message, row] = value.T
+                    for parity in range(2):
+                        for c in range(2):
+                            at = place * 32 + parity * 16 + c * 8
+                            column = c * 256 + slot * 64 if slot < 4 else 512 + c * 64
+                            left[parity, rows, column : column + 64] = turned[message, row][
+                                at : at + 8
+                            ]
+            return carry
+
+        lax.fori_loop(0, 10, turn, 0)
+
+        def part(i, carry):
+            rows = pl.ds(pl.multiple_of(i * 32, 32), 32)
             for parity in range(2):
-                for c in range(2):
-                    high, low = split(main[parity, :, c].reshape(32, 256))
-                    left_high[parity, rows, c * 256 : (c + 1) * 256] = high
-                    left_low[parity, rows, c * 256 : (c + 1) * 256] = low
-                high, low = split(
-                    jnp.concatenate(
-                        [rest[parity, :, 0].reshape(32, 64), rest[parity, :, 1].reshape(32, 64)], 1
-                    )
-                )
-                left_high[parity, rows, 512:640] = high
-                left_low[parity, rows, 512:640] = low
+                high, low = split(left[parity, rows, :])
+                left_high[parity, rows, :] = high
+                left_low[parity, rows, :] = low
             return carry
 
-        lax.fori_loop(0, 10, turn, 0)
+        lax.fori_loop(0, 10, part, 0)
 
         def dot(a, b):
             return jnp.dot(a, b, preferred_element_type=jnp.float32)
@@ -371,12 +476,8 @@
                                 offset + start : offset + start + width,
                             ] = value[row : row + 4]
 
+    wave_all(3).wait_recv()
     wave_all(0).wait_recv()
-    wave_all(1).wait_recv()
-    wave_all(3).wait_recv()
-
-    total = jnp.sum(last[pl.ds(30, 64, stride=LAST), :], axis=0, keepdims=True)
-    sums[grp] = jnp.broadcast_to(total, (8, 128))
 
     def sums_copy(step):
         dest = other_group(step)
@@ -390,9 +491,22 @@
         )
 
     synthesis(0)
+    wave_all(1).wait_recv()
+    synthesis(1)
+
+    shares_all = pltpu.make_async_remote_copy(
+        src_ref=shares.at[pl.ds(0, PEERS - 1)],
+        dst_ref=shares.at[pl.ds(0, PEERS - 1)],
+        send_sem=shares_send_sem,
+        recv_sem=shares_sem,
+        device_id={"grp": grp, "wide": partner(0)},
+        device_id_type=MESH,
+    )
+    shares_all.wait_send()
+    shares_all.wait_recv()
+    sums[grp] = jnp.broadcast_to(jnp.sum(shares[...], axis=0), (8, 128))
     for step in (1, 2, 3):
         sums_copy(step).start()
-    synthesis(1)
     sums_all = pltpu.make_async_remote_copy(
         src_ref=sums.at[0:3],
         dst_ref=sums.at[0:3],
@@ -406,19 +520,16 @@
     sums_out[...] = sums[...]
     wave_all(2).wait_recv()
     synthesis(2)
+    for chunk in range(3):
+        coeffs_all(chunk).wait_send()
     for chunk in range(4):
-        coeffs_all(chunk).wait_send()
         wave_all(chunk).wait_send()
 
 
 def local(spectral, legendre, pair_table, field_map):
     table = jnp.swapaxes(legendre, 1, 2)
-    table_end = jnp.pad(table[:, :, 640:641], ((0, 0), (0, 0), (0, 127)))
-    by_slot = pair_table.reshape(PEERS, 5).T.reshape(-1, 1)
-    pairs_down = jnp.broadcast_to(by_slot, (320, 128))
     smem = pl.BlockSpec(memory_space=pltpu.SMEM)
     vmem = pl.BlockSpec(memory_space=pltpu.VMEM)
-    anywhere = pl.BlockSpec(memory_space=pl.ANY)
     dma = pltpu.SemaphoreType.DMA
     grid, sums = pl.pallas_call(
         kernel,
@@ -427,10 +538,12 @@
             jax.ShapeDtypeStruct((2, 10, 48, LON), jnp.float32),
             jax.ShapeDtypeStruct((GROUPS, 8, 128), jnp.float32),
         ),
-        in_specs=[smem, smem, vmem, anywhere, anywhere, vmem],
+        in_specs=[smem, smem, vmem, pl.BlockSpec(memory_space=pltpu.HBM)],
         out_specs=(vmem, vmem),
         scratch_shapes=[
+            pltpu.VMEM((5, 320, 641), jnp.float32),
             pltpu.VMEM((6, 5, 320, 128), jnp.float32),
+            pltpu.VMEM((320, 128), jnp.int32),
             pltpu.VMEM((5, 320, 768), jnp.bfloat16),
             pltpu.VMEM((5, 320, 768), jnp.bfloat16),
             pltpu.VMEM((GROUPS, 15, 16, 768), jnp.float32),
@@ -443,24 +556,29 @@
             pltpu.VMEM((2, HALF, HALF), jnp.bfloat16),
             pltpu.VMEM((2, 320, HALF), jnp.bfloat16),
             pltpu.VMEM((2, 320, HALF), jnp.bfloat16),
-            pltpu.VMEM((3, 8, 128), jnp.float32),
+            pltpu.VMEM((2, 320, HALF), jnp.float32),
+            pltpu.VMEM((12, 8, 128), jnp.float32),
+            pltpu.VMEM((1, 1, 128), jnp.float32),
+            pltpu.VMEM((PEERS, 1, 128), jnp.float32),
             pltpu.VMEM((GROUPS, 8, 128), jnp.float32),
             dma((6,)),
+            dma((3,)),
+            dma((3,)),
             dma((4,)),
             dma((4,)),
-            dma((4,)),
-            dma((4,)),
+            dma,
+            dma,
             dma,
             dma,
         ],
         compiler_params=pltpu.CompilerParams(
             collective_id=0, has_side_effects=True, vmem_limit_bytes=58 * 2**20
         ),
-    )(pair_table, field_map, spectral, table, table_end, pairs_down)
+    )(pair_table, field_map, spectral, table)
     grid = jnp.swapaxes(grid, 1, 2)
-    by_part = sums[:, 0, :].reshape(GROUPS, 2, 4, 2, 2, 4)
-    chunks = jnp.stack([by_part[:, 0, :, 0], by_part[:, 0, :, 1], by_part[:, 1, :, 0]], 1)
-    checksums = jnp.transpose(chunks, (0, 3, 2, 1, 4)).reshape(8, 48) * (1.0 / LAT)
+    by_step = sums[:, 0, 0:96].reshape(GROUPS, GROUPS, 3, 2, 4)
+    by_group = jnp.stack([jnp.roll(by_step[group], group, 0) for group in range(GROUPS)])
+    checksums = jnp.transpose(by_group, (0, 3, 1, 2, 4)).reshape(8, 48) * (1.0 / LAT)
     return grid, checksums
 
 

time: 154 us -> 146 us (0.948)
  Pallas kernels: 141 us -> 135 us
    pallas_call x1, Pallas kernels: 141 us -> 135 us  [local(): pl.pallas_call(kernel, name='transform', out_shape=(jax.ShapeDtypeStruct(...]
    slice x2 -> x11, local copies, waits for them, and re-layouts: 1.94 us -> 3.73 us  [the longest x9 2.94 us: local(): jnp.roll(by_step[group], group, 0)]
where the time goes in v2:
time: 146 us; the launch traced here: 145 us
  Pallas kernels  135 us (92%)
  local copies, waits for them, and re-layouts  9.45 us (6%)
    pallas_call x1, Pallas kernels, local(): pl.pallas_call(kernel, name='transform', out_shape=(jax.ShapeDtypeStruct(...  135 us
    unnamed x1, local copies, waits for them, and re-layouts  5 us
    slice x9, local copies, waits for them, and re-layouts, local(): jnp.roll(by_step[group], group, 0)  2.94 us

profile of v2, /device:TPU:1, one launch (start us, length us, event | category | flops | bytes accessed | tf_op | source)
XLA Modules:
  0.0 145.3 jit_solution(18279527469190685743)
XLA Ops:
  0.6 135.1 %transform.1 = (f32[2,10,48,1280]{3,2,1,0:T(8,128)}, f32[4,8,128]{2,1,0:T(8,128)}) custom-call(s32[320]{0:T(512)} %pair.1, s32[8]{0:T(128)} %fields.1, f32[8,12,5,2,641]{4,3,2,1,0:T(2,128)} %spectral.1, f32[5,320,641]{2,1,0:T(8,128)} %bitcast.10), custom_call_target="tpu_custom_call" | custom-call | tf_op jit(solution)/shard_map/transform/pallas_call | solution.py:534
  135.8 0.8 slice_reduce_fusion.4
  136.5 0.1 slice.70
  136.6 0.9 slice_reduce_fusion.3
  137.5 0.1 slice.72
  137.6 0.1 slice.74
  137.7 0.8 slice_reduce_fusion.5
  138.4 0.1 slice.68
  138.6 0.1 slice.76
  138.7 0.1 slice.78
  138.8 0.7 slice_reduce_fusion.6
  139.5 0.1 slice.66
  139.6 0.7 mul.15
  140.3 5.0 %copy.8 = f32[2,48,10,1280]{3,1,2,0:T(8,128)} copy(f32[2,48,10,1280]{3,1,2,0:T(8,128)} %bitcast.11) | data formatting | bytes 9830400
  (4 shorter events, 0.1 us)

commit v3 on v2

--- a/solution.py
+++ b/solution.py
@@ -48,6 +48,7 @@
     left_high,
     left_low,
     left,
+    grid,
     energy,
     shares_send,
     shares,
@@ -61,6 +62,7 @@
     shares_sem,
     sums_send_sem,
     sums_sem,
+    out_sem,
 ):
     grp = lax.axis_index("grp")
     wide = lax.axis_index("wide")
@@ -404,6 +406,12 @@
 
     lax.fori_loop(0, 10, make_synthesis, 0)
 
+    def out_copy(first, width):
+        columns = pl.ds(first, width)
+        return pltpu.make_async_copy(
+            grid.at[:, :, :, columns], out.at[:, :, :, columns], out_sem.at[first // 128]
+        )
+
     def place_of(q, dx, slot):
         if dx == 0 and q < 2:
             return {0: (3, 0, q), 1: (3, 1, q), 2: (3, 2, q), 3: (3, 2, 2 + q), 4: (3, q, 3)}[slot]
@@ -414,7 +422,7 @@
             return (q, dx - 1, 3)
         return (q, 3 if slot == f else slot, dx - 1)
 
-    def synthesis(q):
+    def gather(q, messages):
         def turn(lat, carry):
             turned = {}
             for dx in range(GROUPS):
@@ -422,6 +430,8 @@
                 rows = pl.ds(pl.multiple_of(lat * 32 + group * 8, 8), 8)
                 for slot in range(5):
                     message, row, place = place_of(q, dx, slot)
+                    if message not in messages:
+                        continue
                     if (message, row) not in turned:
                         if message < 3:
                             value = waves[message, pl.ds(row * 10 + lat, 64, stride=ROWS), :]
@@ -439,6 +449,7 @@
 
         lax.fori_loop(0, 10, turn, 0)
 
+    def synthesis(q):
         def part(i, carry):
             rows = pl.ds(pl.multiple_of(i * 32, 32), 32)
             for parity in range(2):
@@ -469,12 +480,14 @@
                         for j in range(2):
                             row = lat * 32 + g * 8 + j * 4
                             level = g * 12 + q * 4
-                            out[
+                            grid[
                                 j,
                                 place,
                                 level : level + 4,
                                 offset + start : offset + start + width,
                             ] = value[row : row + 4]
+                if q == 2:
+                    out_copy(offset + start, width).start()
 
     wave_all(3).wait_recv()
     wave_all(0).wait_recv()
@@ -490,9 +503,12 @@
             device_id_type=MESH,
         )
 
+    gather(0, (3, 0))
     synthesis(0)
     wave_all(1).wait_recv()
+    gather(1, (3, 1))
     synthesis(1)
+    gather(2, (3, 0, 1))
 
     shares_all = pltpu.make_async_remote_copy(
         src_ref=shares.at[pl.ds(0, PEERS - 1)],
@@ -519,11 +535,15 @@
     sums_all.wait_recv()
     sums_out[...] = sums[...]
     wave_all(2).wait_recv()
+    gather(2, (2,))
     synthesis(2)
     for chunk in range(3):
         coeffs_all(chunk).wait_send()
     for chunk in range(4):
         wave_all(chunk).wait_send()
+    for start, width in ((0, 256), (256, 256), (512, 128)):
+        for offset in (0, HALF):
+            out_copy(offset + start, width).wait()
 
 
 def local(spectral, legendre, pair_table, field_map):
@@ -539,7 +559,7 @@
             jax.ShapeDtypeStruct((GROUPS, 8, 128), jnp.float32),
         ),
         in_specs=[smem, smem, vmem, pl.BlockSpec(memory_space=pltpu.HBM)],
-        out_specs=(vmem, vmem),
+        out_specs=(pl.BlockSpec(memory_space=pltpu.HBM), vmem),
         scratch_shapes=[
             pltpu.VMEM((5, 320, 641), jnp.float32),
             pltpu.VMEM((6, 5, 320, 128), jnp.float32),
@@ -557,6 +577,7 @@
             pltpu.VMEM((2, 320, HALF), jnp.bfloat16),
             pltpu.VMEM((2, 320, HALF), jnp.bfloat16),
             pltpu.VMEM((2, 320, HALF), jnp.float32),
+            pltpu.VMEM((2, 10, 48, LON), jnp.float32),
             pltpu.VMEM((12, 8, 128), jnp.float32),
             pltpu.VMEM((1, 1, 128), jnp.float32),
             pltpu.VMEM((PEERS, 1, 128), jnp.float32),
@@ -570,6 +591,7 @@
             dma,
             dma,
             dma,
+            dma((10,)),
         ],
         compiler_params=pltpu.CompilerParams(
             collective_id=0, has_side_effects=True, vmem_limit_bytes=58 * 2**20

time: 146 us -> 145 us (level)
  no operation moved by 1% of the time
where the time goes in v3:
time: 145 us; the launch traced here: 144 us
  Pallas kernels  134 us (92%)
  local copies, waits for them, and re-layouts  9.45 us (7%)
    pallas_call x1, Pallas kernels, local(): pl.pallas_call(kernel, name='transform', out_shape=(jax.ShapeDtypeStruct(...  134 us
    unnamed x1, local copies, waits for them, and re-layouts  5 us
    slice x9, local copies, waits for them, and re-layouts, local(): jnp.roll(by_step[group], group, 0)  2.94 us

profile of v3, /device:TPU:1, one launch (start us, length us, event | category | flops | bytes accessed | tf_op | source)
XLA Modules:
  0.0 144.0 jit_solution(14762594767801524559)
XLA Ops:
  0.6 133.7 %transform.1 = (f32[2,10,48,1280]{3,2,1,0:T(8,128)}, f32[4,8,128]{2,1,0:T(8,128)}) custom-call(s32[320]{0:T(512)} %pair.1, s32[8]{0:T(128)} %fields.1, f32[8,12,5,2,641]{4,3,2,1,0:T(2,128)} %spectral.1, f32[5,320,641]{2,1,0:T(8,128)} %bitcast.10), custom_call_target="tpu_custom_call" | custom-call | tf_op jit(solution)/shard_map/transform/pallas_call | solution.py:554
  134.4 0.8 slice_reduce_fusion.4
  135.2 0.1 slice.70
  135.2 0.9 slice_reduce_fusion.3
  136.1 0.1 slice.72
  136.2 0.1 slice.74
  136.3 0.8 slice_reduce_fusion.5
  137.1 0.1 slice.68
  137.2 0.1 slice.76
  137.3 0.1 slice.78
  137.4 0.7 slice_reduce_fusion.6
  138.1 0.1 slice.66
  138.3 0.7 mul.15
  139.0 5.0 %copy.8 = f32[2,48,10,1280]{3,1,2,0:T(8,128)} copy(f32[2,48,10,1280]{3,1,2,0:T(8,128)} %bitcast.11) | data formatting | bytes 9830400
  (4 shorter events, 0.1 us)

commit v4 on v2

--- a/solution.py
+++ b/solution.py
@@ -30,7 +30,7 @@
     fields,
     spectral,
     table_hbm,
-    out,
+    grid,
     sums_out,
     table_whole,
     table,
@@ -414,7 +414,7 @@
             return (q, dx - 1, 3)
         return (q, 3 if slot == f else slot, dx - 1)
 
-    def synthesis(q):
+    def gather(q, messages):
         def turn(lat, carry):
             turned = {}
             for dx in range(GROUPS):
@@ -422,6 +422,8 @@
                 rows = pl.ds(pl.multiple_of(lat * 32 + group * 8, 8), 8)
                 for slot in range(5):
                     message, row, place = place_of(q, dx, slot)
+                    if message not in messages:
+                        continue
                     if (message, row) not in turned:
                         if message < 3:
                             value = waves[message, pl.ds(row * 10 + lat, 64, stride=ROWS), :]
@@ -439,6 +441,7 @@
 
         lax.fori_loop(0, 10, turn, 0)
 
+    def synthesis(q):
         def part(i, carry):
             rows = pl.ds(pl.multiple_of(i * 32, 32), 32)
             for parity in range(2):
@@ -469,7 +472,7 @@
                         for j in range(2):
                             row = lat * 32 + g * 8 + j * 4
                             level = g * 12 + q * 4
-                            out[
+                            grid[
                                 j,
                                 place,
                                 level : level + 4,
@@ -490,9 +493,12 @@
             device_id_type=MESH,
         )
 
+    gather(0, (3, 0))
     synthesis(0)
     wave_all(1).wait_recv()
+    gather(1, (3, 1))
     synthesis(1)
+    gather(2, (3, 0, 1))
 
     shares_all = pltpu.make_async_remote_copy(
         src_ref=shares.at[pl.ds(0, PEERS - 1)],
@@ -517,8 +523,19 @@
     )
     sums_all.wait_send()
     sums_all.wait_recv()
-    sums_out[...] = sums[...]
+    for group in range(GROUPS):
+        row = sums[group, 0:1, :] * (1.0 / LAT)
+        for j in range(2):
+            placed = jnp.zeros((1, 128), jnp.float32)
+            for step in range(GROUPS):
+                for q in range(3):
+                    source = (step * 3 + q) * 8 + j * 4
+                    sink = ((group + step) % GROUPS) * 12 + q * 4
+                    moved = pltpu.roll(row, (sink - source) % 128, 1) if sink != source else row
+                    placed = jnp.where((lane >= sink) & (lane < sink + 4), moved, placed)
+            sums_out[2 * group + j : 2 * group + j + 1, :] = placed[:, 0:48]
     wave_all(2).wait_recv()
+    gather(2, (2,))
     synthesis(2)
     for chunk in range(3):
         coeffs_all(chunk).wait_send()
@@ -526,19 +543,29 @@
         wave_all(chunk).wait_send()
 
 
+def put_out(grid, sums, out, sums_out, sem):
+    copies = [pltpu.make_async_copy(grid.at[j], out.at[j], sem.at[j]) for j in range(2)]
+    for copy in copies:
+        copy.start()
+    sums_out[...] = sums[...]
+    for copy in copies:
+        copy.wait()
+
+
 def local(spectral, legendre, pair_table, field_map):
     table = jnp.swapaxes(legendre, 1, 2)
     smem = pl.BlockSpec(memory_space=pltpu.SMEM)
     vmem = pl.BlockSpec(memory_space=pltpu.VMEM)
+    hbm = pl.BlockSpec(memory_space=pltpu.HBM)
     dma = pltpu.SemaphoreType.DMA
     grid, sums = pl.pallas_call(
         kernel,
         name="transform",
         out_shape=(
             jax.ShapeDtypeStruct((2, 10, 48, LON), jnp.float32),
-            jax.ShapeDtypeStruct((GROUPS, 8, 128), jnp.float32),
+            jax.ShapeDtypeStruct((8, 48), jnp.float32),
         ),
-        in_specs=[smem, smem, vmem, pl.BlockSpec(memory_space=pltpu.HBM)],
+        in_specs=[smem, smem, vmem, hbm],
         out_specs=(vmem, vmem),
         scratch_shapes=[
             pltpu.VMEM((5, 320, 641), jnp.float32),
@@ -572,14 +599,22 @@
             dma,
         ],
         compiler_params=pltpu.CompilerParams(
-            collective_id=0, has_side_effects=True, vmem_limit_bytes=58 * 2**20
+            collective_id=0, has_side_effects=True, vmem_limit_bytes=46 * 2**20
         ),
     )(pair_table, field_map, spectral, table)
-    grid = jnp.swapaxes(grid, 1, 2)
-    by_step = sums[:, 0, 0:96].reshape(GROUPS, GROUPS, 3, 2, 4)
-    by_group = jnp.stack([jnp.roll(by_step[group], group, 0) for group in range(GROUPS)])
-    checksums = jnp.transpose(by_group, (0, 3, 1, 2, 4)).reshape(8, 48) * (1.0 / LAT)
-    return grid, checksums
+    grid, checksums = pl.pallas_call(
+        put_out,
+        name="put_out",
+        out_shape=(
+            jax.ShapeDtypeStruct((2, 10, 48, LON), jnp.float32),
+            jax.ShapeDtypeStruct((8, 48), jnp.float32),
+        ),
+        in_specs=[vmem, vmem],
+        out_specs=(hbm, vmem),
+        scratch_shapes=[dma((2,))],
+        compiler_params=pltpu.CompilerParams(vmem_limit_bytes=2**20),
+    )(grid, sums)
+    return jnp.swapaxes(grid, 1, 2), checksums
 
 
 def solution(mesh):

time: 146 us -> 138 us (0.945)
  local copies, waits for them, and re-layouts: 9.45 us -> 3.16 us
  Pallas kernels: 135 us -> 133 us
    pallas_call x1, Pallas kernels: 135 us -> 130 us  [local(): pl.pallas_call(kernel, name='transform', out_shape=(jax.ShapeDtypeStruct(...]
    slice x11 -> x0, local copies, waits for them, and re-layouts: 3.73 us -> none  [the longest x9 2.94 us: local(): jnp.roll(by_step[group], group, 0)]
    pallas_call x0 -> x1, Pallas kernels: none -> 2.86 us  [local(): pl.pallas_call(put_out, name='put_out', out_shape=(jax.ShapeDtypeStruct((...]
    unnamed x1 -> x6, local copies, waits for them, and re-layouts: 5 us -> 3.16 us
where the time goes in v4:
time: 138 us; the launch traced here: 137 us
  Pallas kernels  133 us (96%)
  local copies, waits for them, and re-layouts  3.16 us (2%)
    pallas_call x1, Pallas kernels, local(): pl.pallas_call(kernel, name='transform', out_shape=(jax.ShapeDtypeStruct(...  130 us
    unnamed x6, local copies, waits for them, and re-layouts  3.16 us
    pallas_call x1, Pallas kernels, local(): pl.pallas_call(put_out, name='put_out', out_shape=(jax.ShapeDtypeStruct((...  2.86 us

profile of v4, /device:TPU:1, one launch (start us, length us, event | category | flops | bytes accessed | tf_op | source)
XLA Modules:
  0.0 137.1 jit_solution(4892189318187901599)
XLA Ops:
  0.6 0.0 copy-start
  0.6 1.8 %copy-done = f32[8,12,5,2,641]{4,3,2,1,0:T(2,128)S(1)} copy-done((f32[8,12,5,2,641]{4,3,2,1,0:T(2,128)S(1)}, f32[8,12,5,2,641]{4,3,2,1,0:T(2,128)}, u32[]{:S(2)}) %copy-start) | copy-done | bytes 2461464
  2.5 0.0 copy-start.1
  2.5 0.7 copy-done.1
  3.1 0.0 copy-start.2
  3.1 0.7 copy-done.2
  3.8 130.5 %transform.1 = (f32[2,10,48,1280]{3,2,1,0:T(8,128)S(1)}, f32[8,48]{1,0:T(8,128)S(1)}) custom-call(s32[320]{0:T(512)S(1)} %copy-done.1, s32[8]{0:T(128)S(1)} %copy-done.2, f32[8,12,5,2,641]{4,3,2,1,0:T(2,128)S(1)} %copy-done, f32[5,320,641]{2,1,0:T(8,128)} %bitcast.2), custom_call_target="tpu_custom_call" | custom-call | tf_op jit(solution)/shard_map/transform/pallas_call | solution.py:561
  134.3 2.9 %put_out.1 = (f32[2,10,48,1280]{3,2,1,0:T(8,128)}, f32[8,48]{1,0:T(8,128)}) custom-call(f32[2,10,48,1280]{3,2,1,0:T(8,128)S(1)} %get-tuple-element.6.grid, f32[8,48]{1,0:T(8,128)S(1)} %get-tuple-element.7.sums), custom_call_target="tpu_custom_call" | custom-call | tf_op jit(solution)/shard_map/put_out/pallas_call | solution.py:605
Async XLA Ops:
  0.6 1.8 %copy-start = (f32[8,12,5,2,641]{4,3,2,1,0:T(2,128)S(1)}, f32[8,12,5,2,641]{4,3,2,1,0:T(2,128)}, u32[]{:S(2)}) copy-start(f32[8,12,5,2,641]{4,3,2,1,0:T(2,128)} %spectral.1) | copy-start | bytes 7384324
  2.5 0.7 copy-start.1
  3.1 0.7 copy-start.2

commit v5 on v4

--- a/solution.py
+++ b/solution.py
@@ -28,10 +28,11 @@
 def kernel(
     pair,
     fields,
-    spectral,
+    spectral_hbm,
     table_hbm,
     grid,
     sums_out,
+    spectral,
     table_whole,
     table,
     pairs_down,
@@ -52,6 +53,7 @@
     shares_send,
     shares,
     sums,
+    first_sem,
     table_sem,
     coeffs_send_sem,
     coeffs_sem,
@@ -85,6 +87,12 @@
         return dest + (dest // 32) * (95 - 2 * dest)
 
     barrier = pltpu.get_barrier_semaphore()
+    first_copies = [
+        pltpu.make_async_copy(source, sink, first_sem.at[i])
+        for i, (source, sink) in enumerate(((spectral_hbm, spectral),))
+    ]
+    for copy in first_copies:
+        copy.start()
     table_copies = [
         pltpu.make_async_copy(
             table_hbm.at[:, :, tile * 128 : (tile + 1) * 128],
@@ -125,6 +133,8 @@
                     ]
         return carry
 
+    for copy in first_copies:
+        copy.wait()
     lax.fori_loop(0, 5, reorder, 0)
 
     def coeffs_copy(chunk, step):
@@ -544,7 +554,12 @@
 
 
 def put_out(grid, sums, out, sums_out, sem):
-    copies = [pltpu.make_async_copy(grid.at[j], out.at[j], sem.at[j]) for j in range(2)]
+    copies = [
+        pltpu.make_async_copy(
+            grid.at[i // 5, pl.ds(i % 5 * 2, 2)], out.at[i // 5, pl.ds(i % 5 * 2, 2)], sem.at[i]
+        )
+        for i in range(10)
+    ]
     for copy in copies:
         copy.start()
     sums_out[...] = sums[...]
@@ -562,12 +577,13 @@
         kernel,
         name="transform",
         out_shape=(
-            jax.ShapeDtypeStruct((2, 10, 48, LON), jnp.float32),
-            jax.ShapeDtypeStruct((8, 48), jnp.float32),
+            pltpu.VMEM((2, 10, 48, LON), jnp.float32),
+            pltpu.VMEM((8, 48), jnp.float32),
         ),
-        in_specs=[smem, smem, vmem, hbm],
+        in_specs=[smem, smem, hbm, hbm],
         out_specs=(vmem, vmem),
         scratch_shapes=[
+            pltpu.VMEM((8, 12, 5, 2, 641), jnp.float32),
             pltpu.VMEM((5, 320, 641), jnp.float32),
             pltpu.VMEM((6, 5, 320, 128), jnp.float32),
             pltpu.VMEM((320, 128), jnp.int32),
@@ -588,6 +604,7 @@
             pltpu.VMEM((1, 1, 128), jnp.float32),
             pltpu.VMEM((PEERS, 1, 128), jnp.float32),
             pltpu.VMEM((GROUPS, 8, 128), jnp.float32),
+            dma((3,)),
             dma((6,)),
             dma((3,)),
             dma((3,)),
@@ -599,7 +616,7 @@
             dma,
         ],
         compiler_params=pltpu.CompilerParams(
-            collective_id=0, has_side_effects=True, vmem_limit_bytes=46 * 2**20
+            collective_id=0, has_side_effects=True, vmem_limit_bytes=50 * 2**20
         ),
     )(pair_table, field_map, spectral, table)
     grid, checksums = pl.pallas_call(
@@ -611,7 +628,7 @@
         ),
         in_specs=[vmem, vmem],
         out_specs=(hbm, vmem),
-        scratch_shapes=[dma((2,))],
+        scratch_shapes=[dma((10,))],
         compiler_params=pltpu.CompilerParams(vmem_limit_bytes=2**20),
     )(grid, sums)
     return jnp.swapaxes(grid, 1, 2), checksums

time: 138 us -> 136 us (0.986)
  local copies, waits for them, and re-layouts: 3.16 us -> 0 us
    unnamed x6 -> x0, local copies, waits for them, and re-layouts: 3.16 us -> none
where the time goes in v5:
time: 136 us; the launch traced here: 134 us
  Pallas kernels  134 us (99%)
    pallas_call x1, Pallas kernels, local(): pl.pallas_call(kernel, name='transform', out_shape=(pltpu.VMEM((2, 10, 48...  131 us
    pallas_call x1, Pallas kernels, local(): pl.pallas_call(put_out, name='put_out', out_shape=(jax.ShapeDtypeStruct((...  2.92 us

profile of v5, /device:TPU:1, one launch (start us, length us, event | category | flops | bytes accessed | tf_op | source)
XLA Modules:
  0.0 134.1 jit_solution(14873270842327336191)
XLA Ops:
  0.6 130.6 %transform.1 = (f32[2,10,48,1280]{3,2,1,0:T(8,128)S(1)}, f32[8,48]{1,0:T(8,128)S(1)}) custom-call(s32[320]{0:T(512)} %pair.1, s32[8]{0:T(128)} %fields.1, f32[8,12,5,2,641]{4,3,2,1,0:T(2,128)} %spectral_hbm.1, f32[5,320,641]{2,1,0:T(8,128)} %bitcast.2), custom_call_target="tpu_custom_call" | custom-call | tf_op jit(solution)/shard_map/transform/pallas_call | solution.py:576
  131.2 2.9 %put_out.1 = (f32[2,10,48,1280]{3,2,1,0:T(8,128)}, f32[8,48]{1,0:T(8,128)}) custom-call(f32[2,10,48,1280]{3,2,1,0:T(8,128)S(1)} %get-tuple-element.6.grid, f32[8,48]{1,0:T(8,128)S(1)} %get-tuple-element.7.sums), custom_call_target="tpu_custom_call" | custom-call | tf_op jit(solution)/shard_map/put_out/pallas_call | solution.py:622
